TPU v7x, 64 devices: a 2x2x8 block of a 4x4x8 slice. The times are simulated.
64 devices in a mesh: rep: 8 (over x, y, core), dp: 8 (over z).
Axes of the slice: x: 2, y: 2, z: 8, core: 2. Of those that a mesh axis runs over, the one named last changes fastest.
The devices are a block of a 4x4x8 slice.
Arguments:
- x: bfloat16 [64, 2048, 768], P(('rep', 'dp')), parts along dimension 0
- dy: bfloat16 [64, 2048, 768], P(('rep', 'dp')), parts along dimension 0
- w_gate: bfloat16 [2, 768, 2048], replicated
- w_up: bfloat16 [2, 768, 2048], replicated
- w_down: bfloat16 [2, 2048, 768], replicated
- m_w_gate: float32 [2, 768, 2048], P(None, 'dp')
- m_w_up: float32 [2, 768, 2048], P(None, 'dp')
- m_w_down: float32 [2, 2048, 768], P(None, 'dp')
- v_w_gate: float32 [2, 768, 2048], P(None, 'dp')
- v_w_up: float32 [2, 768, 2048], P(None, 'dp')
- v_w_down: float32 [2, 2048, 768], P(None, 'dp')
Outputs:
- output 1: bfloat16 [16, 768, 2048], P('rep'), parts along dimension 0
- output 2: bfloat16 [16, 768, 2048], P('rep'), parts along dimension 0
- output 3: bfloat16 [16, 2048, 768], P('rep'), parts along dimension 0
- output 4: float32 [16, 768, 2048], P('rep', 'dp'), parts along dimension 0
- output 5: float32 [16, 768, 2048], P('rep', 'dp'), parts along dimension 0
- output 6: float32 [16, 2048, 768], P('rep', 'dp'), parts along dimension 0
- output 7: float32 [16, 768, 2048], P('rep', 'dp'), parts along dimension 0
- output 8: float32 [16, 768, 2048], P('rep', 'dp'), parts along dimension 0
- output 9: float32 [16, 2048, 768], P('rep', 'dp'), parts along dimension 0
There are 8 independent parts. A program takes and returns all parts, laid end to end along the dimension named above; an argument that names none is the same for every part.
All inputs are finite; a program needn't handle non-finite values.
Results may differ from a plain program's by a relative error of at most 0.022.
Values are sent between devices in bfloat16 or wider.
A program may use at most 768 MiB of HBM per device.

v0:
```python
import jax
import jax.numpy as jnp
from jax import lax

NAMES = ("w_gate", "w_up", "w_down")


def matmul(a, w):
    return jnp.dot(a, w, preferred_element_type=jnp.float32).astype(jnp.bfloat16)


def normed(h):
    wide = h.astype(jnp.float32)
    scale = lax.rsqrt(jnp.mean(wide**2, -1, keepdims=True) + 1e-6)
    return (wide * scale).astype(jnp.bfloat16)


def layer(h, w):
    a = normed(h)
    gate = jnp.dot(a, w["w_gate"], preferred_element_type=jnp.float32)
    up = jnp.dot(a, w["w_up"], preferred_element_type=jnp.float32)
    return h + matmul((jax.nn.silu(gate) * up).astype(jnp.bfloat16), w["w_down"])


def adamw(w, m, v, g):
    m = 0.9 * m + 0.1 * g
    v = 0.95 * v + 0.05 * g * g
    step = m * lax.rsqrt(v + 1e-8) + 0.1 * w
    return (w - 0.02 * step).astype(jnp.bfloat16), m, v


def clipped(gradients, sum_of_squares, count):
    factor = jnp.minimum(1.0, 0.5 * lax.rsqrt(sum_of_squares / count + 1e-30))
    return [g * factor for g in gradients]


def stack(weights, h):
    for number in range(weights["w_gate"].shape[0]):
        h = layer(h, {name: w[number] for name, w in weights.items()})
    return h


def solution(mesh):
    groups = mesh.shape["rep"]

    def step(x, dy, *arrays):
        weights, m, v = (arrays[i : i + 3] for i in (0, 3, 6))
        x, dy = (t.reshape(groups, -1, *t.shape[1:]) for t in (x, dy))

        def of_a_group(x, dy):
            _, back = jax.vjp(lambda w: stack(w, x), dict(zip(NAMES, weights, strict=True)))
            by_weights = back(dy)[0]
            gradients = [by_weights[name].astype(jnp.float32) for name in NAMES]
            gradients = clipped(gradients, sum(jnp.sum(g * g) for g in gradients), sum(g.size for g in gradients))
            new = [adamw(w.astype(jnp.float32), m, v, g) for w, m, v, g in zip(weights, m, v, gradients, strict=True)]
            return tuple(one[which] for which in range(3) for one in new)

        return tuple(t.reshape(-1, *t.shape[2:]) for t in jax.vmap(of_a_group)(x, dy))

    return step
```

profile of v0, /device:TPU:22, one launch (start us, length us, event | category | flops | bytes accessed | tf_op | source)
XLA Modules:
  0.0 861.0 jit_solution(11964184211805252111)
XLA Ops:
  23.5 14.2 %fusion.73 = f32[2048,2048]{1,0:T(8,128)} fusion(bf16[2,768,2048]{2,1,0:T(8,128)(2,1)} %param.3, bf16[1,2048,768]{2,1,0:T(8,128)(2,1)S(1)} %copy-done.1, f32[2048]{0:T(1024)S(1)} %add_rsqrt_fusion), kind=kOutput, calls=%fused_computation.86 | convolution fusion | flops 6447169536 | bytes 23076864 | tf_op jit(solution)/vmap(jvp())/dot_general | solution.py:21
  46.4 10.8 %fusion.39 = (f32[2048]{0:T(1024)S(1)}, bf16[1,1,2048,768]{2,3,1,0:T(8,128)(2,1)S(1)}) fusion(bf16[2048,2048]{1,0:T(8,128)(2,1)S(1)} %fusion.26, bf16[2,2048,768]{2,1,0:T(8,128)(2,1)} %param.4, bf16[1,2048,768]{1,2,0:T(8,128)(2,1)S(1)} %copy-done.7), kind=kOutput, calls=%fused_computation.56 | convolution fusion | flops 6450313216 | bytes 17833984 | tf_op jit(solution)/vmap(jvp())/dot_general | solution.py:9
  57.2 13.3 %fusion.63 = f32[2048,2048]{1,0:T(8,128)} fusion(bf16[2,768,2048]{2,1,0:T(8,128)(2,1)} %param, bf16[1,1,2048,768]{2,3,1,0:T(8,128)(2,1)S(1)} %get-tuple-element.10, f32[2048]{0:T(1024)S(1)} %bitcast.359), kind=kOutput, calls=%fused_computation.75 | convolution fusion | flops 6447169536 | bytes 23076864 | tf_op jit(solution)/vmap(jvp())/dot_general | solution.py:20
  70.5 12.3 %fusion.66 = f32[2048,2048]{1,0:T(8,128)} fusion(bf16[2,768,2048]{2,1,0:T(8,128)(2,1)} %param.3, bf16[1,1,2048,768]{2,3,1,0:T(8,128)(2,1)S(1)} %get-tuple-element.10, f32[2048]{0:T(1024)S(1)} %bitcast.360), kind=kOutput, calls=%fused_computation.78 | convolution fusion | flops 6447169536 | bytes 23076864 | tf_op jit(solution)/vmap(jvp())/dot_general | solution.py:21
  82.8 9.5 %convolution_convert_fusion.1 = bf16[2048,2048]{1,0:T(8,128)(2,1)} fusion(bf16[1,2048,768]{2,1,0:T(8,128)(2,1)S(1)} %copy-done.5, bf16[2,2048,768]{2,1,0:T(8,128)(2,1)S(1)} %bitcast.355), kind=kOutput, calls=%fused_computation.51 | convolution fusion | flops 6446645248 | bytes 14680064 | tf_op jit(solution)/vmap(transpose(jvp()))/dot_general | solution.py:9
  95.5 15.0 %fusion.6 = bf16[2048,2048]{1,0:T(8,128)(2,1)S(1)} fusion(f32[2048,2048]{1,0:T(8,128)} %fusion.63, f32[2048,2048]{1,0:T(8,128)} %fusion.66, bf16[2048,2048]{1,0:T(8,128)(2,1)} %convolution_convert_fusion.1), kind=kLoop, calls=%fused_computation.11 | loop fusion | flops 50331648 | bytes 50331648
  113.7 9.5 %convolution_convert_fusion.2 = bf16[2048,768]{0,1:T(8,128)(2,1)} fusion(bf16[2048,2048]{1,0:T(8,128)(2,1)S(1)} %fusion.6, bf16[2,768,2048]{2,1,0:T(8,128)(2,1)} %param), kind=kOutput, calls=%fused_computation.66 | convolution fusion | flops 6442450944 | bytes 14680064 | tf_op jit(solution)/vmap(transpose(jvp()))/dot_general | solution.py:20
  123.2 17.7 %fusion.41 = (f32[2048]{0:T(1024)S(1)}, bf16[2048,768]{0,1:T(8,128)(2,1)}) fusion(bf16[1,1,2048,768]{2,3,1,0:T(8,128)(2,1)} %copy-done.9, bf16[2048,768]{0,1:T(8,128)(2,1)} %convolution_convert_fusion.2, bf16[2,768,2048]{2,1,0:T(8,128)(2,1)} %param.3, bf16[2048,2048]{1,0:T(8,128)(2,1)} %convolution_convert_fusion.1, f32[2048,2048]{1,0:T(8,128)} %fusion.63), kind=kOutput, calls=%fused_computation.58 | convolution fusion | flops 6477051904 | bytes 37756928 | tf_op jit(solution)/vmap(transpose(jvp()))/dot_general | solution.py:21
  147.6 11.0 %convolution_bitcast_fusion = f32[1,2048,768]{2,1,0:T(8,128)} fusion(bf16[2048,2048]{1,0:T(8,128)(2,1)} %copy-done.2, bf16[2048,768]{0,1:T(8,128)(2,1)S(1)} %fusion.60), kind=kOutput, calls=%fused_computation.64 | convolution fusion | flops 6442450944 | bytes 17825792 | tf_op jit(solution)/vmap(transpose(jvp()))/dot_general | solution.py:9
  160.6 16.3 %fusion.42 = f32[1,2048,768]{2,1,0:T(8,128)} fusion(f32[2048,2048]{1,0:T(8,128)} %fusion.66, f32[2048,2048]{1,0:T(8,128)} %fusion.63, bf16[1,2048,768]{2,1,0:T(8,128)(2,1)S(1)} %copy-done.6), kind=kOutput, calls=%fused_computation.60 | convolution fusion | flops 6467616768 | bytes 42991616 | tf_op jit(solution)/vmap(transpose(jvp()))/dot_general | solution.py:9
  177.0 9.8 %convolution_convert_fusion = bf16[2048,2048]{1,0:T(8,128)(2,1)S(1)} fusion(bf16[2048,768]{0,1:T(8,128)(2,1)} %copy-done.11, bf16[2,2048,768]{2,1,0:T(8,128)(2,1)} %param.4), kind=kOutput, calls=%fused_computation.50 | convolution fusion | flops 6446645248 | bytes 14680064 | tf_op jit(solution)/vmap(transpose(jvp()))/dot_general | solution.py:9
  190.1 12.2 %fusion.51 = f32[1,768,2048]{2,1,0:T(8,128)} fusion(bf16[2048,2048]{1,0:T(8,128)(2,1)S(1)} %convolution_convert_fusion, f32[2048,2048]{1,0:T(8,128)} %copy-done, bf16[1,2048,768]{1,2,0:T(8,128)(2,1)S(1)} %copy-done.8, f32[2048]{0:T(1024)S(1)} %copy-done.14), kind=kOutput, calls=%fused_computation.63 | convolution fusion | flops 6472335360 | bytes 34611200 | tf_op jit(solution)/vmap(transpose(jvp()))/dot_general | solution.py:21
  202.4 14.5 %fusion.45 = f32[1,768,2048]{2,1,0:T(8,128)} fusion(bf16[2048,2048]{1,0:T(8,128)(2,1)} %convolution_convert_fusion.1, f32[2048,2048]{1,0:T(8,128)} %fusion.63, bf16[1,1,2048,768]{2,3,1,0:T(8,128)(2,1)} %copy-done.9, f32[2048]{0:T(1024)S(1)} %bitcast.362), kind=kOutput, calls=%fused_computation.61 | convolution fusion | flops 6472335360 | bytes 34611200 | tf_op jit(solution)/vmap(transpose(jvp()))/dot_general | solution.py:21
  217.0 20.3 %fusion.48 = f32[1,768,2048]{2,1,0:T(8,128)} fusion(f32[2048,2048]{1,0:T(8,128)} %copy-done, f32[2048,2048]{1,0:T(8,128)} %fusion.73, bf16[2048,2048]{1,0:T(8,128)(2,1)} %copy-done.16, bf16[1,2048,768]{1,2,0:T(8,128)(2,1)S(1)} %copy-done.8, f32[2048]{0:T(1024)S(1)} %copy-done.14), kind=kOutput, calls=%fused_computation.62 | convolution fusion | flops 6493306880 | bytes 51388416 | tf_op jit(solution)/vmap(transpose(jvp()))/dot_general | solution.py:20
  239.2 10.7 %convolution_bitcast_fusion.1 = f32[1,768,2048]{2,1,0:T(8,128)} fusion(bf16[2048,2048]{1,0:T(8,128)(2,1)} %copy-done.3, bf16[1,1,2048,768]{2,3,1,0:T(8,128)(2,1)S(1)} %copy-done.10, f32[2048]{0:T(1024)S(1)} %bitcast.363), kind=kOutput, calls=%fused_computation.65 | convolution fusion | flops 6447169536 | bytes 17833984 | tf_op jit(solution)/vmap(transpose(jvp()))/dot_general | solution.py:20
  253.0 54.3 %reduce-scatter.27.cloned.1.call-done = f32[1,256,768]{2,1,0:T(8,128)} async-done(((f32[1,2048,768]{2,1,0:T(8,128)}), f32[1,256,768]{2,1,0:T(8,128)}) %reduce-scatter.27.cloned.1.call-update) | async-done | bytes 786448
  309.5 71.2 %reduce-scatter.25.cloned.1.call-done = f32[1,96,2048]{2,1,0:T(8,128)} async-done(((f32[1,768,2048]{2,1,0:T(8,128)}), f32[1,96,2048]{2,1,0:T(8,128)}) %reduce-scatter.25.cloned.1.call-update) | async-done | bytes 786448
  381.9 71.5 %reduce-scatter.23.cloned.1.call-done = f32[1,96,2048]{2,1,0:T(8,128)} async-done(((f32[1,768,2048]{2,1,0:T(8,128)}), f32[1,96,2048]{2,1,0:T(8,128)}) %reduce-scatter.23.cloned.1.call-update) | async-done | bytes 786448
  455.6 71.1 %reduce-scatter.21.cloned.1.call-done = f32[1,96,2048]{2,1,0:T(8,128)} async-done(((f32[1,768,2048]{2,1,0:T(8,128)}), f32[1,96,2048]{2,1,0:T(8,128)}) %reduce-scatter.21.cloned.1.call-update) | async-done | bytes 786448
  527.8 72.1 %reduce-scatter.19.cloned.1.call-done = f32[1,96,2048]{2,1,0:T(8,128)} async-done(((f32[1,768,2048]{2,1,0:T(8,128)}), f32[1,96,2048]{2,1,0:T(8,128)}) %reduce-scatter.19.cloned.1.call-update) | async-done | bytes 786448
  604.1 16.7 %all-reduce.16 = f32[1]{0:T(128)} all-reduce(f32[1]{0:T(128)} %bitcast.50), channel_id=5, replica_groups=mesh['rep'=8,'dp'=8] {'dp'}, use_global_device_ids=true, to_apply=%region_3.4.clone | all-reduce | flops 1 | bytes 8 | tf_op jit(solution)/vmap()/reduce_sum | solution.py:54
  636.2 61.3 %all-gather.14.cloned.1.call-done = bf16[1,2,2048,768]{3,2,1,0:T(8,128)(2,1)} async-done(((bf16[1,2,256,768]{3,2,1,0:T(8,128)(2,1)}), bf16[1,2,2048,768]{3,2,1,0:T(8,128)(2,1)}) %all-gather.14.cloned.1.call-update) | async-done | bytes 6291472 | tf_op jit(solution)/reshape | solution.py:58
  697.4 71.8 %all-gather.12.cloned.1.call-done = bf16[1,2,768,2048]{3,2,1,0:T(8,128)(2,1)} async-done(((bf16[1,2,96,2048]{3,2,1,0:T(8,128)(2,1)}), bf16[1,2,768,2048]{3,2,1,0:T(8,128)(2,1)}) %all-gather.12.cloned.1.call-update) | async-done | bytes 6291472 | tf_op jit(solution)/reshape | solution.py:58
  769.2 71.8 %all-gather.10.cloned.1.call-done = bf16[1,2,768,2048]{3,2,1,0:T(8,128)(2,1)} async-done(((bf16[1,2,96,2048]{3,2,1,0:T(8,128)(2,1)}), bf16[1,2,768,2048]{3,2,1,0:T(8,128)(2,1)}) %all-gather.10.cloned.1.call-update) | async-done | bytes 6291472 | tf_op jit(solution)/reshape | solution.py:58
  (89 shorter events, 84.3 us)
Async XLA Ops:
  7.2 7.5 copy-start.1
  7.2 244.6 %reduce-scatter.29.cloned.1.call-start = ((), (), s32[]{:S(2)}) async-start(), calls=%async_computation.14 | async-start | bytes 7077888
  14.6 8.9 %copy-start.13 = (f32[2048]{0:T(1024)}, f32[2048]{0:T(1024)S(1)}, u32[]{:S(2)}) copy-start(f32[2048]{0:T(1024)S(1)} %add_rsqrt_fusion) | copy-start | bytes 24580
  23.5 14.2 %copy-start = (f32[2048,2048]{1,0:T(8,128)}, f32[2048,2048]{1,0:T(8,128)S(1)}, u32[]{:S(2)}) copy-start(f32[2048,2048]{1,0:T(8,128)S(1)} %fusion.75) | copy-start | bytes 50331652
  37.7 8.6 %copy-start.7 = (bf16[1,2048,768]{1,2,0:T(8,128)(2,1)S(1)}, bf16[1,2048,768]{1,2,0:T(8,128)(2,1)}, u32[]{:S(2)}) copy-start(bf16[1,2048,768]{1,2,0:T(8,128)(2,1)} %copy) | copy-start | bytes 9437188
  46.3 10.8 %copy-start.2 = (bf16[2048,2048]{1,0:T(8,128)(2,1)}, bf16[2048,2048]{1,0:T(8,128)(2,1)S(1)}, u32[]{:S(2)}) copy-start(bf16[2048,2048]{1,0:T(8,128)(2,1)S(1)} %fusion.26) | copy-start | bytes 25165828
  57.2 13.3 %copy-start.9 = (bf16[1,1,2048,768]{2,3,1,0:T(8,128)(2,1)}, bf16[1,1,2048,768]{2,3,1,0:T(8,128)(2,1)S(1)}, u32[]{:S(2)}) copy-start(bf16[1,1,2048,768]{2,3,1,0:T(8,128)(2,1)S(1)} %get-tuple-element.10) | copy-start | bytes 9437188
  57.2 25.6 %slice-start.2 = ((s8[6291456]{0:T(1024)(128)(4,1)}), s8[4194304]{0:T(1024)(128)(4,1)S(1)}, s32[]{:S(2)}) async-start(s8[6291456]{0:T(1024)(128)(4,1)} %bitcast.354), calls=%async_computation.17 | async-start | bytes 8388608
  70.5 12.3 %copy-start.5 = (bf16[1,2048,768]{2,1,0:T(8,128)(2,1)S(1)}, bf16[1,2048,768]{2,1,0:T(8,128)(2,1)}, u32[]{:S(2)}) copy-start(bf16[1,2048,768]{2,1,0:T(8,128)(2,1)} %param.5) | copy-start | bytes 9437188
  70.5 12.3 %slice-start.3 = ((s8[6291456]{0:T(1024)(128)(4,1)}), s8[2097152]{0:T(1024)(128)(4,1)S(1)}, s32[]{:S(2)}) async-start(s8[6291456]{0:T(1024)(128)(4,1)} %bitcast.354), calls=%async_computation.18 | async-start | bytes 4194304
  158.7 148.6 %reduce-scatter.27.cloned.1.call-start = ((), (), s32[]{:S(2)}) async-start(), calls=%async_computation.13 | async-start | bytes 7077888
  177.0 13.1 %copy-start.8 = (bf16[1,2048,768]{1,2,0:T(8,128)(2,1)S(1)}, bf16[1,2048,768]{1,2,0:T(8,128)(2,1)}, u32[]{:S(2)}) copy-start(bf16[1,2048,768]{1,2,0:T(8,128)(2,1)} %copy) | copy-start | bytes 9437188
  177.0 13.1 %copy-start.14 = (f32[2048]{0:T(1024)S(1)}, f32[2048]{0:T(1024)}, u32[]{:S(2)}) copy-start(f32[2048]{0:T(1024)} %copy-done.13) | copy-start | bytes 24580
  177.0 203.7 %reduce-scatter.25.cloned.1.call-start = ((), (), s32[]{:S(2)}) async-start(), calls=%async_computation.12 | async-start | bytes 7077888
  186.8 3.2 copy-start.16
  202.3 251.1 %reduce-scatter.23.cloned.1.call-start = ((), (), s32[]{:S(2)}) async-start(), calls=%async_computation.11 | async-start | bytes 7077888
  216.9 309.7 %reduce-scatter.21.cloned.1.call-start = ((), (), s32[]{:S(2)}) async-start(), calls=%async_computation.10 | async-start | bytes 7077888
  237.4 362.5 %reduce-scatter.19.cloned.1.call-start = ((), (), s32[]{:S(2)}) async-start(), calls=%async_computation.9 | async-start | bytes 7077888
  250.0 447.5 %all-gather.14.cloned.1.call-start = ((), (), s32[]{:S(2)}) async-start(), calls=%async_computation.8 | async-start | bytes 7077888 | tf_op jit(solution)/reshape | solution.py:58
  626.4 5.3 copy-start.12
  626.4 142.8 %all-gather.12.cloned.1.call-start = ((), (), s32[]{:S(2)}) async-start(), calls=%async_computation.7 | async-start | bytes 7077888 | tf_op jit(solution)/reshape | solution.py:58
  631.6 209.5 %all-gather.10.cloned.1.call-start = ((), (), s32[]{:S(2)}) async-start(), calls=%async_computation.6 | async-start | bytes 7077888 | tf_op jit(solution)/reshape | solution.py:58
  841.1 7.1 copy-start.4
  841.1 9.9 %slice-start = ((s8[6291456]{0:T(1024)(128)(4,1)}), s8[4194304]{0:T(1024)(128)(4,1)S(1)}, s32[]{:S(2)}) async-start(s8[6291456]{0:T(1024)(128)(4,1)} %bitcast.349), calls=%async_computation.15 | async-start | bytes 8388608
  (6 other events, 12.5 us)
Sparse Core Ops, SparseCore 0:
  158.8 75.5 reduce-scatter.28
  236.8 70.4 reduce-scatter.26
  310.2 70.4 reduce-scatter.24
  382.9 70.4 reduce-scatter.22
  456.2 70.4 reduce-scatter.20
  529.4 70.4 reduce-scatter.18
  626.6 70.8 all-gather.13
  699.6 69.5 all-gather.11
  771.4 69.5 all-gather.9
where the time goes:
time: 870 us; the launch traced here: 861 us
  waiting for transfers between devices  546 us (63%)
  matrix products  191 us (22%)
  other arithmetic  55.8 us (6%)
  local copies, waits for them, and re-layouts  33.6 us (4%)
  between operations  17.9 us (2%)
  blocking collectives  16.7 us (2%)
    unnamed x15, waiting for transfers between devices  341 us
    reshape x3, waiting for transfers between devices, step(): t.reshape(-1, *t.shape[2:])  205 us
    dot_general x5, matrix products, layer(): up = jnp.dot(a, w['w_up'], preferred_element_type=jnp.float32)  70.8 us
    dot_general x5, matrix products, layer(): gate = jnp.dot(a, w['w_gate'], preferred_element_type=jnp.float32)  62.6 us
    dot_general x5, matrix products, matmul(): jnp.dot(a, w, preferred_element_type=jnp.float32).astype(jnp.bfloat16)  57.4 us
    unnamed x47, local copies, waits for them, and re-layouts  33 us
    unnamed x5, other arithmetic  28.6 us
  transfers between devices with their start and end apart: 9, of which 8 were waited for; matrix products, arithmetic and copies ran while one was open for 12% of the time, Pallas kernels for 0%

commit v1 on v0

v1 whole, which is shorter than its diff:
```python
import functools

import jax
import jax.numpy as jnp
from jax import lax
from jax.experimental import pallas as pl
from jax.experimental.pallas import tpu as pltpu
from jax.sharding import PartitionSpec as P

NAMES = ("w_gate", "w_up", "w_down")
MESH = pl.DeviceIdType.MESH
F32, BF16 = jnp.float32, jnp.bfloat16


def matmul(a, w):
    return jnp.dot(a, w, preferred_element_type=F32).astype(BF16)


def normed(h):
    wide = h.astype(F32)
    scale = lax.rsqrt(jnp.mean(wide**2, -1, keepdims=True) + 1e-6)
    return (wide * scale).astype(BF16)


def layer(h, w):
    a = normed(h)
    gate = jnp.dot(a, w["w_gate"], preferred_element_type=F32)
    up = jnp.dot(a, w["w_up"], preferred_element_type=F32)
    return h + matmul((jax.nn.silu(gate) * up).astype(BF16), w["w_down"])


def stack(weights, h):
    for number in range(weights["w_gate"].shape[0]):
        h = layer(h, {name: w[number] for name, w in weights.items()})
    return h


def update_kernel(n, layers, count, *refs):
    ssq, g, w, m, v = refs[0], refs[1:4], refs[4:7], refs[7:10], refs[10:13]
    nw, nm, nv = refs[13:16], refs[16:19], refs[19:22]
    gs, ws, ms, vs = refs[22:25], refs[25:28], refs[28:31], refs[31:34]
    slots, load_sem, store_sem, own_sem, ssq_send, ssq_recv, send_sem, recv_sem = refs[34:]
    me = lax.axis_index("dp")
    right, left = lax.rem(me + 1, n), lax.rem(me + n - 1, n)
    blocks = [(i, l) for l in range(layers) for i in range(3)]
    rows = [r.shape[1] for r in g]

    loads = {}
    for k, (i, l) in enumerate(blocks):
        own = pl.ds(pl.multiple_of(me * rows[i], rows[i]), rows[i])
        pairs = ((g[i].at[l], gs[i].at[l]), (w[i].at[l, own], ws[i].at[l]), (m[i].at[l], ms[i].at[l]), (v[i].at[l], vs[i].at[l]))
        loads[k] = [pltpu.make_async_copy(src, dst, load_sem.at[k, j]) for j, (src, dst) in enumerate(pairs)]
        for copy in loads[k]:
            copy.start()

    barrier = pltpu.get_barrier_semaphore()
    for d in range(1, n):
        pl.semaphore_signal(barrier, inc=1, device_id={"dp": lax.rem(me + d, n)}, device_id_type=MESH)
    pl.semaphore_wait(barrier, n - 1)

    sums = [
        pltpu.make_async_remote_copy(
            src_ref=ssq, dst_ref=slots.at[d], send_sem=ssq_send.at[d], recv_sem=ssq_recv.at[d],
            device_id={"dp": lax.rem(me + d, n)}, device_id_type=MESH,
        )
        for d in range(1, n)
    ]
    for copy in sums:
        copy.start()
    total = ssq[...]
    for d, copy in enumerate(sums, 1):
        copy.wait()
        total = total + slots[d]
    total = jnp.sum(jnp.sum(total, axis=1, keepdims=True), axis=0, keepdims=True)
    factor = jnp.minimum(1.0, 0.5 * lax.rsqrt(total / count + 1e-30))

    def piece(ref, i, l, owner, way):
        half = rows[i] // 2
        return ref.at[l, pl.ds(pl.multiple_of(owner * rows[i] + way * half, half), half)]

    def hop(k, way, step, first):
        i, l = blocks[k]
        owner = lax.rem(me + (n - step if way == 0 else step), n)
        half = rows[i] // 2
        src = ws[i].at[l, pl.ds(way * half, half)] if first else piece(nw[i], i, l, owner, way)
        return pltpu.make_async_remote_copy(
            src_ref=src, dst_ref=piece(nw[i], i, l, owner, way), send_sem=send_sem.at[way, k, step], recv_sem=recv_sem.at[way, k, step],
            device_id={"dp": (right, left)[way]}, device_id_type=MESH,
        )

    stores = []
    for k, (i, l) in enumerate(blocks):
        for copy in loads[k]:
            copy.wait()
        tile = 32

        def body(t, _, i=i, l=l, tile=tile):
            at = (l, pl.ds(pl.multiple_of(t * tile, tile), tile))
            grad = gs[i][at].astype(F32) * factor
            wide = ws[i][at].astype(F32)
            new_m = 0.9 * ms[i][at] + 0.1 * grad
            new_v = 0.95 * vs[i][at] + 0.05 * grad * grad
            ms[i][at] = new_m
            vs[i][at] = new_v
            step = new_m * lax.rsqrt(new_v + 1e-8) + 0.1 * wide
            ws[i][at] = (wide - 0.02 * step).astype(BF16)
            return 0

        lax.fori_loop(0, rows[i] // tile, body, 0)
        for way in range(2):
            hop(k, way, 0, True).start()
        own = pl.ds(pl.multiple_of(me * rows[i], rows[i]), rows[i])
        pairs = ((ws[i].at[l], nw[i].at[l, own]), (ms[i].at[l], nm[i].at[l]), (vs[i].at[l], nv[i].at[l]))
        for j, (src, dst) in enumerate(pairs):
            stores.append(pltpu.make_async_copy(src, dst, store_sem.at[k, j]))
            stores[-1].start()

    for step in range(1, n):
        for k in range(len(blocks)):
            for way in range(2):
                hop(k, way, step - 1, False).wait_recv()
                if step < n - 1:
                    hop(k, way, step, False).start()
    for step in range(n - 1):
        for k in range(len(blocks)):
            for way in range(2):
                hop(k, way, step, step == 0).wait_send()
    for copy in stores:
        copy.wait()


def update(n, ssq, g, w, m, v):
    layers = w[0].shape[0]
    count = float(sum(t.size for t in w))
    blocks = 3 * layers
    anywhere = pl.BlockSpec(memory_space=pl.ANY)
    outs = pl.pallas_call(
        functools.partial(update_kernel, n, layers, count),
        out_shape=[jax.ShapeDtypeStruct(t.shape, t.dtype) for t in (*w, *m, *v)],
        in_specs=[pl.BlockSpec(memory_space=pltpu.VMEM)] + [anywhere] * 12,
        out_specs=[anywhere] * 9,
        scratch_shapes=[pltpu.VMEM(t.shape, t.dtype) for t in (*g, *g, *m, *v)]
        + [
            pltpu.VMEM((n, *ssq.shape), F32),
            pltpu.SemaphoreType.DMA((blocks, 4)),
            pltpu.SemaphoreType.DMA((blocks, 3)),
            pltpu.SemaphoreType.DMA((1,)),
            pltpu.SemaphoreType.DMA((n,)),
            pltpu.SemaphoreType.DMA((n,)),
            pltpu.SemaphoreType.DMA((2, blocks, n - 1)),
            pltpu.SemaphoreType.DMA((2, blocks, n - 1)),
        ],
        compiler_params=pltpu.CompilerParams(collective_id=1, has_side_effects=True, vmem_limit_bytes=40 * 2**20),
        name="update",
    )(ssq, *g, *w, *m, *v)
    return tuple(outs)


def solution(mesh):
    n = mesh.shape["dp"]

    def device(x, dy, *arrays):
        w, m, v = (arrays[i : i + 3] for i in (0, 3, 6))
        _, back = jax.vjp(lambda w: stack(w, x[0]), dict(zip(NAMES, w, strict=True)))
        by_weights = back(dy[0])[0]
        g = [lax.psum_scatter(by_weights[name], "dp", scatter_dimension=1, tiled=True) for name in NAMES]
        ssq = sum(jnp.sum(jnp.square(t.astype(F32))) for t in g)
        ssq = jnp.zeros((8, 128), F32).at[0, 0].set(ssq)
        return update(n, ssq, g, w, m, v)

    whole, part = P(None, None, None), P(None, "dp", None)
    return jax.shard_map(
        device,
        mesh=mesh,
        in_specs=(P(("rep", "dp")), P(("rep", "dp"))) + (whole,) * 3 + (part,) * 6,
        out_specs=(P("rep"),) * 3 + (P("rep", "dp"),) * 6,
        check_vma=False,
    )
```

time: 870 us -> 639 us (0.73)
  waiting for transfers between devices: 546 us -> 148 us
  Pallas kernels: 0 us -> 190 us
  other arithmetic: 55.8 us -> 26.2 us
  matrix products: 191 us -> 213 us
  blocking collectives: 16.7 us -> 0 us
    unnamed x15 -> x3, waiting for transfers between devices: 341 us -> 0.16 us
    reshape x3 -> x0, waiting for transfers between devices: 205 us -> none  [step(): t.reshape(-1, *t.shape[2:])]
    pallas_call x0 -> x1, Pallas kernels: none -> 190 us  [update(): pl.pallas_call(functools.partial(update_kernel, n, layers, count), out_sh...]
    reduce_scatter x0 -> x3, waiting for transfers between devices: none -> 148 us  [device(): lax.psum_scatter(by_weights[name], 'dp', scatter_dimension=1, tiled=True)]
    unnamed x5 -> x1, other arithmetic: 28.6 us -> 0.01 us
    dot_general x15, matrix products: 191 us -> 213 us  [the longest x5 80.9 us: layer(): gate = jnp.dot(a, w['w_gate'], preferred_element_type=F32)]
    add_any x0 -> x4, other arithmetic: none -> 19.1 us  [the longest x3 14.1 us: stack(): h = layer(h, {name: w[number] for name, w in weights.items()})]
    reduce_sum x1 -> x0, blocking collectives: 16.7 us -> none  [of_a_group(): jnp.sum(g * g)]
  transfers between devices with their start and end apart: 9 -> 3, of which waited for: 8 -> 3; matrix products, arithmetic and copies ran while one was open for 12% -> 12% of each run, Pallas kernels for 0% -> 0%
where the time goes in v1:
time: 639 us; the launch traced here: 632 us
  matrix products  213 us (33%)
  Pallas kernels  190 us (30%)
  waiting for transfers between devices  148 us (23%)
  local copies, waits for them, and re-layouts  38 us (6%)
  other arithmetic  26.2 us (4%)
  between operations  16.1 us (3%)
    pallas_call x1, Pallas kernels, update(): pl.pallas_call(functools.partial(update_kernel, n, layers, count), out_sh...  190 us
    reduce_scatter x3, waiting for transfers between devices, device(): lax.psum_scatter(by_weights[name], 'dp', scatter_dimension=1, tiled=True)  148 us
    dot_general x5, matrix products, layer(): gate = jnp.dot(a, w['w_gate'], preferred_element_type=F32)  80.9 us
    dot_general x5, matrix products, layer(): up = jnp.dot(a, w['w_up'], preferred_element_type=F32)  71.9 us
    dot_general x5, matrix products, matmul(): return jnp.dot(a, w, preferred_element_type=F32).astype(BF16)  60.4 us
    unnamed x49, local copies, waits for them, and re-layouts  38 us
    add_any x3, other arithmetic, stack(): h = layer(h, {name: w[number] for name, w in weights.items()})  14.1 us
  transfers between devices with their start and end apart: 3, of which 3 were waited for; matrix products, arithmetic and copies ran while one was open for 12% of the time, Pallas kernels for 0%

profile of v1, /device:TPU:22, one launch (start us, length us, event | category | flops | bytes accessed | tf_op | source)
XLA Modules:
  0.0 631.6 jit_solution(11039038596486134356)
XLA Ops:
  11.2 5.0 copy.21
  16.2 11.6 %convolution_convert_fusion.1 = bf16[2048,2048]{1,0:T(8,128)(2,1)} fusion(bf16[1,2048,768]{2,1,0:T(8,128)(2,1)} %param.14, bf16[2,2048,768]{2,1,0:T(8,128)(2,1)} %refs_6_.1), kind=kOutput, calls=%fused_computation.32 | convolution fusion | flops 6446645248 | bytes 14680064 | tf_op jit(solution)/shard_map/transpose(jvp())/dot_general | solution.py:16
  27.7 11.8 %fusion.44 = f32[2048,2048]{1,0:T(8,128)} fusion(bf16[2,768,2048]{2,1,0:T(8,128)(2,1)} %refs_4_.1, bf16[1,2048,768]{2,1,0:T(8,128)(2,1)S(1)} %copy-done.7, f32[2048]{0:T(1024)S(1)} %add_rsqrt_fusion), kind=kOutput, calls=%fused_computation.68 | convolution fusion | flops 6447169536 | bytes 23076864 | tf_op jit(solution)/shard_map/jvp()/dot_general | solution.py:27
  39.5 16.9 %multiply_convert_fusion.1 = (bf16[2048,2048]{1,0:T(8,128)(2,1)}, f32[2048,2048]{1,0:T(8,128)}) fusion(f32[2048,2048]{1,0:T(8,128)} %fusion.44, bf16[2,768,2048]{2,1,0:T(8,128)(2,1)} %refs_5_.1, bf16[1,2048,768]{2,1,0:T(8,128)(2,1)} %param.13, f32[2048]{0:T(1024)S(1)} %add_rsqrt_fusion), kind=kOutput, calls=%fused_computation.17 | convolution fusion | flops 6472335360 | bytes 48242688 | tf_op jit(solution)/shard_map/jvp()/dot_general | solution.py:28
  56.4 10.9 %fusion.19 = (f32[2048]{0:T(1024)S(1)}, bf16[2048,768]{0,1:T(8,128)(2,1)S(1)}) fusion(bf16[2048,2048]{1,0:T(8,128)(2,1)} %get-tuple-element.21, bf16[2,2048,768]{2,1,0:T(8,128)(2,1)} %refs_6_.1, bf16[1,2048,768]{1,2,0:T(8,128)(2,1)S(1)} %copy.20), kind=kOutput, calls=%fused_computation.37 | convolution fusion | flops 6450313216 | bytes 17833984 | tf_op jit(solution)/shard_map/jvp()/dot_general | solution.py:16
  69.0 12.1 %fusion.37 = f32[2048,2048]{1,0:T(8,128)} fusion(bf16[2,768,2048]{2,1,0:T(8,128)(2,1)} %refs_5_.1, bf16[2048,768]{0,1:T(8,128)(2,1)S(1)} %get-tuple-element.24, f32[2048]{0:T(1024)S(1)} %fusion.79), kind=kOutput, calls=%fused_computation.61 | convolution fusion | flops 6447169536 | bytes 23076864 | tf_op jit(solution)/shard_map/jvp()/dot_general | solution.py:28
  81.2 25.9 %fusion.2 = (bf16[2048,2048]{1,0:T(8,128)(2,1)}, f32[2048,2048]{1,0:T(8,128)}) fusion(f32[2048,2048]{1,0:T(8,128)} %fusion.37, bf16[2048,2048]{1,0:T(8,128)(2,1)} %convolution_convert_fusion.1, bf16[2,768,2048]{2,1,0:T(8,128)(2,1)} %refs_4_.1, bf16[2048,768]{0,1:T(8,128)(2,1)} %copy-done.10, f32[2048]{0:T(1024)S(1)} %fusion.79), kind=kOutput, calls=%fused_computation.8 | convolution fusion | flops 6497501184 | bytes 56631296 | tf_op jit(solution)/shard_map/jvp()/dot_general | solution.py:27
  107.0 12.1 %convolution_convert_fusion.2 = bf16[2048,768]{0,1:T(8,128)(2,1)} fusion(bf16[2048,2048]{1,0:T(8,128)(2,1)} %get-tuple-element.25, bf16[2,768,2048]{2,1,0:T(8,128)(2,1)} %refs_4_.1), kind=kOutput, calls=%fused_computation.46 | convolution fusion | flops 6442450944 | bytes 14680064 | tf_op jit(solution)/shard_map/transpose(jvp())/dot_general | solution.py:27
  119.1 13.1 %fusion.58 = bf16[1,768,2048]{2,1,0:T(8,128)(2,1)} fusion(bf16[2048,2048]{1,0:T(8,128)(2,1)} %convolution_convert_fusion.1, bf16[2048,768]{0,1:T(8,128)(2,1)S(1)} %copy-done.11, f32[2048]{0:T(1024)S(1)} %fusion.79, f32[2048,2048]{1,0:T(8,128)} %get-tuple-element.26), kind=kOutput, calls=%fused_computation.79 | convolution fusion | flops 6473908224 | bytes 31465472 | tf_op jit(solution)/shard_map/transpose(jvp())/dot_general | solution.py:28
  132.2 17.7 %fusion.21 = (f32[2048]{0:T(1024)S(1)}, bf16[2048,768]{0,1:T(8,128)(2,1)}) fusion(bf16[2048,768]{0,1:T(8,128)(2,1)} %copy-done.10, bf16[2048,768]{0,1:T(8,128)(2,1)} %convolution_convert_fusion.2, bf16[2,768,2048]{2,1,0:T(8,128)(2,1)} %refs_5_.1, bf16[2048,2048]{1,0:T(8,128)(2,1)} %convolution_convert_fusion.1, f32[2048,2048]{1,0:T(8,128)} %get-tuple-element.26), kind=kOutput, calls=%fused_computation.39 | convolution fusion | flops 6477051904 | bytes 37756928 | tf_op jit(solution)/shard_map/transpose(jvp())/dot_general | solution.py:28
  150.0 5.1 fusion.30
  156.7 11.2 %convolution_convert_fusion = bf16[2048,2048]{1,0:T(8,128)(2,1)} fusion(bf16[2048,768]{0,1:T(8,128)(2,1)S(1)} %fusion.30, bf16[2,2048,768]{2,1,0:T(8,128)(2,1)} %refs_6_.1), kind=kOutput, calls=%fused_computation.31 | convolution fusion | flops 6446645248 | bytes 14680064 | tf_op jit(solution)/shard_map/transpose(jvp())/dot_general | solution.py:16
  167.9 12.0 %fusion.57 = bf16[1,768,2048]{2,1,0:T(8,128)(2,1)S(1)} fusion(bf16[2048,2048]{1,0:T(8,128)(2,1)} %convolution_convert_fusion, f32[2048,2048]{1,0:T(8,128)} %fusion.44, bf16[1,2048,768]{1,2,0:T(8,128)(2,1)S(1)} %copy-done.5, f32[2048]{0:T(1024)S(1)} %copy-done.16), kind=kOutput, calls=%fused_computation.78 | convolution fusion | flops 6473908224 | bytes 31465472 | tf_op jit(solution)/shard_map/transpose(jvp())/dot_general | solution.py:28
  183.1 12.1 %fusion.56 = bf16[1,768,2048]{2,1,0:T(8,128)(2,1)} fusion(bf16[2048,2048]{1,0:T(8,128)(2,1)} %get-tuple-element.25, bf16[2048,768]{0,1:T(8,128)(2,1)} %copy-done.10, f32[2048]{0:T(1024)S(1)} %fusion.79), kind=kOutput, calls=%fused_computation.77 | convolution fusion | flops 6447169536 | bytes 14688256 | tf_op jit(solution)/shard_map/transpose(jvp())/dot_general | solution.py:27
  195.3 19.0 %fusion.50 = bf16[1,768,2048]{2,1,0:T(8,128)(2,1)} fusion(f32[2048,2048]{1,0:T(8,128)} %fusion.44, f32[2048,2048]{1,0:T(8,128)} %get-tuple-element.22, bf16[2048,2048]{1,0:T(8,128)(2,1)} %convolution_convert_fusion, bf16[1,2048,768]{1,2,0:T(8,128)(2,1)S(1)} %copy-done.5, f32[2048]{0:T(1024)S(1)} %copy-done.16), kind=kOutput, calls=%fused_computation.75 | convolution fusion | flops 6494879744 | bytes 48242688 | tf_op jit(solution)/shard_map/transpose(jvp())/dot_general | solution.py:27
  214.3 6.0 pad_add_fusion.2
  220.4 10.9 %fusion.49 = bf16[1,2048,768]{2,1,0:T(8,128)(2,1)S(1)} fusion(bf16[2048,2048]{1,0:T(8,128)(2,1)} %get-tuple-element.21, bf16[2048,768]{0,1:T(8,128)(2,1)} %copy-done.9), kind=kOutput, calls=%fused_computation.74 | convolution fusion | flops 6444023808 | bytes 14680064 | tf_op jit(solution)/shard_map/transpose(jvp())/dot_general | solution.py:16
  231.3 15.8 %fusion.53 = bf16[1,2048,768]{2,1,0:T(8,128)(2,1)} fusion(bf16[1,2048,768]{2,1,0:T(8,128)(2,1)S(1)} %copy-done.8, f32[2048,2048]{1,0:T(8,128)} %fusion.37, f32[2048,2048]{1,0:T(8,128)} %get-tuple-element.26), kind=kOutput, calls=%fused_computation.76 | convolution fusion | flops 6469189632 | bytes 39845888 | tf_op jit(solution)/shard_map/transpose(jvp())/dot_general | solution.py:16
  252.2 6.6 %reduce-scatter.6.cloned.1.call-done.refs_2_ = bf16[2,96,2048]{2,1,0:T(8,128)(2,1)} async-done(((bf16[2,768,2048]{2,1,0:T(8,128)(2,1)}), bf16[2,96,2048]{2,1,0:T(8,128)(2,1)}) %reduce-scatter.6.cloned.1.call-update) | async-done | bytes 786448 | tf_op jit(solution)/shard_map/reduce_scatter | solution.py:166
  260.9 71.3 %reduce-scatter.4.cloned.1.call-done.refs_1_ = bf16[2,96,2048]{2,1,0:T(8,128)(2,1)} async-done(((bf16[2,768,2048]{2,1,0:T(8,128)(2,1)}), bf16[2,96,2048]{2,1,0:T(8,128)(2,1)}) %reduce-scatter.4.cloned.1.call-update) | async-done | bytes 786448 | tf_op jit(solution)/shard_map/reduce_scatter | solution.py:166
  335.6 70.0 %reduce-scatter.8.cloned.1.call-done.refs_3_ = bf16[2,256,768]{2,1,0:T(8,128)(2,1)} async-done(((bf16[2,2048,768]{2,1,0:T(8,128)(2,1)}), bf16[2,256,768]{2,1,0:T(8,128)(2,1)}) %reduce-scatter.8.cloned.1.call-update) | async-done | bytes 786448 | tf_op jit(solution)/shard_map/reduce_scatter | solution.py:166
  411.8 189.9 %update.1 = (bf16[2,768,2048]{2,1,0:T(8,128)(2,1)}, bf16[2,768,2048]{2,1,0:T(8,128)(2,1)}, bf16[2,2048,768]{2,1,0:T(8,128)(2,1)}, f32[2,96,2048]{2,1,0:T(8,128)S...) custom-call(f32[8,128]{1,0:T(8,128)S(1)} %scatter.4.refs_0_, ...), custom_call_target="tpu_custom_call" | custom-call | tf_op jit(solution)/shard_map/update/pallas_call | solution.py:137
  601.7 6.8 %copy.31 = bf16[2,768,2048]{2,1,0:T(8,128)(2,1)} copy(bf16[2,768,2048]{2,1,0:T(8,128)(2,1)} %get-tuple-element.38) | data formatting | bytes 12582912
  608.5 6.8 %copy.32 = bf16[2,768,2048]{2,1,0:T(8,128)(2,1)} copy(bf16[2,768,2048]{2,1,0:T(8,128)(2,1)} %get-tuple-element.39) | data formatting | bytes 12582912
  (63 shorter events, 35.1 us)
Async XLA Ops:
  7.2 251.6 %reduce-scatter.6.cloned.1.call-start = ((), (), s32[]{:S(2)}) async-start(), calls=%async_computation.4 | async-start | bytes 7077888 | tf_op jit(solution)/shard_map/reduce_scatter | solution.py:166
  10.5 46.0 %copy-start.4 = (bf16[1,2048,768]{1,2,0:T(8,128)(2,1)}, bf16[1,2048,768]{1,2,0:T(8,128)(2,1)S(1)}, u32[]{:S(2)}) copy-start(bf16[1,2048,768]{1,2,0:T(8,128)(2,1)S(1)} %copy.20) | copy-start | bytes 9437188
  11.1 28.4 %copy-start.15 = (f32[2048]{0:T(1024)}, f32[2048]{0:T(1024)S(1)}, u32[]{:S(2)}) copy-start(f32[2048]{0:T(1024)S(1)} %add_rsqrt_fusion) | copy-start | bytes 24580
  16.2 11.6 %copy-start.7 = (bf16[1,2048,768]{2,1,0:T(8,128)(2,1)S(1)}, bf16[1,2048,768]{2,1,0:T(8,128)(2,1)}, u32[]{:S(2)}) copy-start(bf16[1,2048,768]{2,1,0:T(8,128)(2,1)} %param.13) | copy-start | bytes 9437188
  67.3 0.6 copy-start.13
  67.3 1.7 copy-start.10
  107.0 12.1 %copy-start.11 = (bf16[2048,768]{0,1:T(8,128)(2,1)S(1)}, bf16[2048,768]{0,1:T(8,128)(2,1)}, u32[]{:S(2)}) copy-start(bf16[2048,768]{0,1:T(8,128)(2,1)} %copy-done.10) | copy-start | bytes 9437188
  132.2 17.7 %copy-start.14 = (f32[2048]{0:T(1024)S(1)}, f32[2048]{0:T(1024)}, u32[]{:S(2)}) copy-start(f32[2048]{0:T(1024)} %copy-done.13) | copy-start | bytes 24580
  132.2 17.7 %copy-start.6 = (bf16[1,2048,768]{1,2,0:T(8,128)(2,1)S(1)}, bf16[1,2048,768]{1,2,0:T(8,128)(2,1)}, u32[]{:S(2)}) copy-start(bf16[1,2048,768]{1,2,0:T(8,128)(2,1)} %copy.21) | copy-start | bytes 9437188
  155.0 1.6 copy-start.9
  156.7 11.2 %copy-start.5 = (bf16[1,2048,768]{1,2,0:T(8,128)(2,1)S(1)}, bf16[1,2048,768]{1,2,0:T(8,128)(2,1)}, u32[]{:S(2)}) copy-start(bf16[1,2048,768]{1,2,0:T(8,128)(2,1)} %copy-done.4) | copy-start | bytes 9437188
  156.7 11.2 %copy-start.16 = (f32[2048]{0:T(1024)S(1)}, f32[2048]{0:T(1024)}, u32[]{:S(2)}) copy-start(f32[2048]{0:T(1024)} %copy-done.15) | copy-start | bytes 24580
  167.9 12.0 %copy-start.12 = (bf16[1,768,2048]{2,1,0:T(8,128)(2,1)S(1)}, bf16[1,768,2048]{2,1,0:T(8,128)(2,1)}, u32[]{:S(2)}) copy-start(bf16[1,768,2048]{2,1,0:T(8,128)(2,1)} %fusion.58) | copy-start | bytes 9437188
  183.0 149.1 %reduce-scatter.4.cloned.1.call-start = ((), (), s32[]{:S(2)}) async-start(), calls=%async_computation.3 | async-start | bytes 7077888 | tf_op jit(solution)/shard_map/reduce_scatter | solution.py:166
  220.3 11.0 %copy-start.8 = (bf16[1,2048,768]{2,1,0:T(8,128)(2,1)S(1)}, bf16[1,2048,768]{2,1,0:T(8,128)(2,1)}, u32[]{:S(2)}) copy-start(bf16[1,2048,768]{2,1,0:T(8,128)(2,1)} %param.14) | copy-start | bytes 9437188
  220.3 185.3 %reduce-scatter.8.cloned.1.call-start = ((), (), s32[]{:S(2)}) async-start(), calls=%async_computation.5 | async-start | bytes 7077888 | tf_op jit(solution)/shard_map/reduce_scatter | solution.py:166
  252.1 156.3 %copy-start.3 = (f32[2,96,2048]{2,1,0:T(8,128)S(1)}, f32[2,96,2048]{2,1,0:T(8,128)}, u32[]{:S(2)}) copy-start(f32[2,96,2048]{2,1,0:T(8,128)} %refs_7_.1) | copy-start | bytes 4718596
  408.4 1.1 copy-start
  409.5 1.1 copy-start.1
  410.7 1.1 copy-start.2
  601.7 13.5 %slice-start = ((s8[6291456]{0:T(1024)(128)(4,1)}), s8[4194304]{0:T(1024)(128)(4,1)S(1)}, s32[]{:S(2)}) async-start(s8[6291456]{0:T(1024)(128)(4,1)} %bitcast.77), calls=%async_computation.6 | async-start | bytes 8388608
  608.5 6.8 %slice-start.1 = ((s8[6291456]{0:T(1024)(128)(4,1)}), s8[2097152]{0:T(1024)(128)(4,1)S(1)}, s32[]{:S(2)}) async-start(s8[6291456]{0:T(1024)(128)(4,1)} %bitcast.77), calls=%async_computation.7 | async-start | bytes 4194304
Sparse Core Ops, SparseCore 0:
  183.2 75.5 reduce-scatter.5
  261.7 70.4 reduce-scatter.3
  335.1 70.4 reduce-scatter.7

commit v2 on v1

--- a/solution.py
+++ b/solution.py
@@ -7,32 +7,321 @@
 from jax.experimental.pallas import tpu as pltpu
 from jax.sharding import PartitionSpec as P
 
-NAMES = ("w_gate", "w_up", "w_down")
 MESH = pl.DeviceIdType.MESH
+STARTS = (4, 8, 12, 16, 16, 16, 20, 22, 24, 26, 26, 26)
 F32, BF16 = jnp.float32, jnp.bfloat16
 
 
-def matmul(a, w):
-    return jnp.dot(a, w, preferred_element_type=F32).astype(BF16)
-
-
-def normed(h):
-    wide = h.astype(F32)
-    scale = lax.rsqrt(jnp.mean(wide**2, -1, keepdims=True) + 1e-6)
-    return (wide * scale).astype(BF16)
-
-
-def layer(h, w):
-    a = normed(h)
-    gate = jnp.dot(a, w["w_gate"], preferred_element_type=F32)
-    up = jnp.dot(a, w["w_up"], preferred_element_type=F32)
-    return h + matmul((jax.nn.silu(gate) * up).astype(BF16), w["w_down"])
-
-
-def stack(weights, h):
-    for number in range(weights["w_gate"].shape[0]):
-        h = layer(h, {name: w[number] for name, w in weights.items()})
-    return h
+def unit_scale(wide):
+    return lax.rsqrt(jnp.mean(wide * wide, -1, keepdims=True) + 1e-6)
+
+
+def nn(a, b):
+    return lax.dot_general(a, b, (((1,), (0,)), ((), ())), preferred_element_type=F32)
+
+
+def nt(a, b):
+    return lax.dot_general(a, b, (((1,), (1,)), ((), ())), preferred_element_type=F32)
+
+
+def gradients_kernel(n, *refs):
+    x, dy, wg, wu, wd, og, ou, od, ossq = refs[:9]
+    h, a, at, d, dt, acc, wgb, wub, wdb, act, dg, du, gg, gu, gd, rgu, rd = refs[9:26]
+    wsem, xsem, osem, send_sem, recv_sem, credit = refs[26:]
+    me = lax.axis_index("dp")
+    right, left = lax.rem(me + 1, n), lax.rem(me + n - 1, n)
+    tokens, width = h.shape
+    hidden = wg.shape[2]
+    chunk = act.shape[1]
+    chunks = hidden // chunk
+    tile = tokens // 4
+    rows, deep = og.shape[1], od.shape[1] // 2
+    wide_cols, half_cols = rgu.shape[-1], rd.shape[-1]
+
+    def tokens_at(i):
+        return pl.ds(pl.multiple_of(i * tile, tile), tile)
+
+    def chunk_of(t):
+        number = jnp.where(lax.div(t, chunks) == 1, 1, 0)
+        cols = pl.ds(pl.multiple_of(lax.rem(t, chunks) * chunk, chunk), chunk)
+        slot = lax.rem(t, 2)
+        return [
+            pltpu.make_async_copy(wg.at[number, :, cols], wgb.at[slot], wsem.at[slot, 0]),
+            pltpu.make_async_copy(wu.at[number, :, cols], wub.at[slot], wsem.at[slot, 1]),
+            pltpu.make_async_copy(wd.at[number, cols, :], wdb.at[slot], wsem.at[slot, 2]),
+        ]
+
+    def next_chunk(t, last):
+        for copy in chunk_of(t):
+            copy.wait()
+
+        @pl.when(t < last)
+        def _():
+            for copy in chunk_of(t + 1):
+                copy.start()
+
+    load_x = pltpu.make_async_copy(x, h, xsem.at[0])
+    load_dy = pltpu.make_async_copy(dy, d, xsem.at[1])
+    load_x.start()
+    for copy in chunk_of(0):
+        copy.start()
+    load_dy.start()
+    barrier = pltpu.get_barrier_semaphore()
+    for neighbour in (left, right):
+        pl.semaphore_signal(barrier, inc=1, device_id={"dp": neighbour}, device_id_type=MESH)
+    load_x.wait()
+
+    def norm_all():
+        def body(i, _):
+            wide = h[tokens_at(i), :].astype(F32)
+            a[tokens_at(i), :] = (wide * unit_scale(wide)).astype(BF16)
+            return 0
+
+        lax.fori_loop(0, 4, body, 0)
+
+    def turn(src, dst, i, size):
+        part = pl.ds(pl.multiple_of(i * size, size), size)
+        dst[:, part] = src[part, :].T
+
+    norm_all()
+    acc[...] = jnp.zeros_like(acc)
+    load_dy.wait()
+
+    def forward(t, _):
+        next_chunk(t, 3 * chunks - 1)
+        slot = lax.rem(t, 2)
+        turn(d, dt, t, tokens // chunks)
+        for i in range(4):
+            part = pl.ds(i * tile, tile)
+            gate = nn(a[part, :], wgb[slot])
+            up = nn(a[part, :], wub[slot])
+            acc[part, :] += nn((gate * jax.nn.sigmoid(gate) * up).astype(BF16), wdb[slot])
+        return 0
+
+    lax.fori_loop(0, chunks, forward, 0)
+
+    def between(i, _):
+        out = (h[tokens_at(i), :].astype(F32) + acc[tokens_at(i), :].astype(BF16).astype(F32)).astype(BF16)
+        h[tokens_at(i), :] = out
+        wide = out.astype(F32)
+        a[tokens_at(i), :] = (wide * unit_scale(wide)).astype(BF16)
+        acc[tokens_at(i), :] = jnp.zeros((tile, width), F32)
+        turn(a, at, i, tile)
+        return 0
+
+    lax.fori_loop(0, 4, between, 0)
+    ossq[...] = jnp.zeros_like(ossq)
+    pl.semaphore_wait(barrier, 2)
+
+    def block(kind, way, j, owner):
+        number = jnp.where(j < 6, 1, 0)
+        part = lax.rem(j, 6)
+        if kind == 0:
+            at_rows = pl.ds(pl.multiple_of(owner * rows, rows), rows)
+            at_cols = pl.ds(pl.multiple_of(part * wide_cols, wide_cols), wide_cols)
+            return (gg, gu)[way].at[number, at_rows, at_cols]
+        at_rows = pl.ds(pl.multiple_of(owner * 2 * deep + (part - 4) * deep, deep), deep)
+        return gd.at[number, at_rows, pl.ds(way * half_cols, half_cols)]
+
+    def landing(kind, way, j, s):
+        part = lax.rem(j, 6)
+        return rgu.at[way, part, s] if kind == 0 else rd.at[way, part - 4, s]
+
+    def hop(kind, way, lane, j, s):
+        owner = lax.rem(me + (n - 1 - s if way == 0 else 1 + s), n)
+        return pltpu.make_async_remote_copy(
+            src_ref=block(kind, way, j, owner), dst_ref=landing(kind, way, j, s),
+            send_sem=send_sem.at[way, lane], recv_sem=recv_sem.at[way, lax.rem(j, 6), s],
+            device_id={"dp": (right, left)[way]}, device_id_type=MESH,
+        )
+
+    def serve(kind, lane, j, s, valid):
+        @pl.when(jnp.logical_and(valid, s == 0))
+        def _():
+            @pl.when(j >= 6)
+            def _():
+                for way in range(2):
+                    pl.semaphore_wait(credit.at[way, lane], 1)
+
+            for way in range(2):
+                hop(kind, way, lane, j, s).start()
+
+        @pl.when(jnp.logical_and(valid, s > 0))
+        def _():
+            for way in range(2):
+                before = hop(kind, way, lane, j, s - 1)
+                before.wait_recv()
+                owner = lax.rem(me + (2 * n - 1 - s if way == 0 else 1 + s), n)
+                ref = block(kind, way, j, owner)
+                ref[...] = (ref[...].astype(F32) + landing(kind, way, j, s - 1)[...].astype(F32)).astype(BF16)
+                before.wait_send()
+
+            @pl.when(s < n - 1)
+            def _():
+                for way in range(2):
+                    hop(kind, way, lane, j, s).start()
+
+            @pl.when(s == n - 1)
+            def _():
+                for way in range(2):
+                    ended = block(kind, way, j, me)[...].astype(F32)
+                    ended = (ended * ended).reshape(-1, 8, ended.shape[-1])
+                    ended = jnp.sum(ended, axis=0)
+                    for c in range(0, ended.shape[-1], 128):
+                        ossq[...] += ended[:, c : c + 128]
+
+                @pl.when(j < 6)
+                def _():
+                    for way in range(2):
+                        pl.semaphore_signal(credit.at[way, lane], inc=1, device_id={"dp": (left, right)[way]}, device_id_type=MESH)
+
+    def lane(which, step):
+        first, second = STARTS[which], STARTS[which + 6]
+        later = step >= second
+        s = step - jnp.where(later, second, first)
+        serve(0 if which < 4 else 1, which, jnp.where(later, which + 6, which), s, jnp.logical_and(s >= 0, s <= n - 1))
+
+    def backward(number, count, rounds):
+        t = chunks + count
+        next_chunk(t, 3 * chunks - 1)
+        slot = lax.rem(t, 2)
+        cols = pl.ds(pl.multiple_of(lax.rem(count, chunks) * chunk, chunk), chunk)
+        for i in range(4):
+            part = pl.ds(i * tile, tile)
+            gate = nn(a[part, :], wgb[slot])
+            up = nn(a[part, :], wub[slot])
+            back = nt(d[part, :], wdb[slot]).astype(BF16).astype(F32)
+            sig = jax.nn.sigmoid(gate)
+            silu = gate * sig
+            act[part, :] = (silu * up).astype(BF16)
+            by_up = (back * silu).astype(BF16)
+            by_gate = (back * up * (sig + silu * (1.0 - sig))).astype(BF16)
+            du[part, :] = by_up
+            dg[part, :] = by_gate
+            if number == 1:
+                acc[part, :] += nt(by_gate, wgb[slot]) + nt(by_up, wub[slot])
+            rounds(i)
+        gg[number, :, cols] = nn(at[...], dg[...]).astype(BF16)
+        rounds(4)
+        gu[number, :, cols] = nn(at[...], du[...]).astype(BF16)
+        rounds(5)
+        gd[number, cols, :] = nn(dt[...], act[...]).T.astype(BF16)
+        rounds(6)
+
+    def last_layer(count, _):
+        def rounds(place):
+            if place not in (0, 4):
+                which = {1: 0, 2: 1, 3: 2, 5: 0, 6: 1}[place]
+                lane(which, 2 * count + (place > 3))
+            if place == 6:
+                lane(2, 2 * count + 1)
+
+        backward(1, count, rounds)
+        return 0
+
+    lax.fori_loop(0, chunks, last_layer, 0)
+    for which in (2, 3, 4, 5):
+        lane(which, 2 * chunks)
+
+    def through_norm(i, _):
+        part = tokens_at(i)
+        wide = h[part, :].astype(F32)
+        scale = unit_scale(wide)
+        by_a = acc[part, :].astype(BF16).astype(F32)
+        by_scale = jnp.sum(by_a * wide, -1, keepdims=True) * (scale * scale * scale) * (-1.0 / width)
+        by_h = (by_a * scale + by_scale * wide).astype(BF16)
+        d[part, :] = (d[part, :].astype(F32) + by_h.astype(F32)).astype(BF16)
+        return 0
+
+    lax.fori_loop(0, 4, through_norm, 0)
+    load_x = pltpu.make_async_copy(x, h, xsem.at[0])
+    load_x.start()
+    for which in (2, 3, 4, 5):
+        lane(which, 2 * chunks + 1)
+    load_x.wait()
+    norm_all()
+
+    def turn_both(i, _):
+        turn(d, dt, i, tile)
+        turn(a, at, i, tile)
+        return 0
+
+    lax.fori_loop(0, 4, turn_both, 0)
+
+    def first_layer(count, _):
+        def rounds(place):
+            which = {0: 2, 1: 3, 2: 4, 3: 5, 5: 0, 6: 1}.get(place)
+            if which is not None:
+                lane(which, chunks + 2 + count)
+
+        backward(0, count, rounds)
+        return 0
+
+    lax.fori_loop(chunks, 2 * chunks, first_layer, 0)
+
+    def rest(step, _):
+        for which in (0, 1, 2, 3, 4, 5):
+            lane(which, step)
+        return 0
+
+    lax.fori_loop(3 * chunks + 2, 3 * chunks + 10, rest, 0)
+
+    own = pl.ds(pl.multiple_of(me * rows, rows), rows)
+    own_deep = pl.ds(pl.multiple_of(me * 2 * deep, 2 * deep), 2 * deep)
+    outs = [
+        pltpu.make_async_copy(gg.at[:, own, :], og, osem.at[0]),
+        pltpu.make_async_copy(gu.at[:, own, :], ou, osem.at[1]),
+        pltpu.make_async_copy(gd.at[:, own_deep, :], od, osem.at[2]),
+    ]
+    for copy in outs:
+        copy.start()
+    for copy in outs:
+        copy.wait()
+
+
+def gradients(n, x, dy, w):
+    wg, wu, wd = w
+    tokens, width = x.shape
+    layers, _, hidden = wg.shape
+    chunk, wide_cols = hidden // 8, hidden // 4
+    rows, deep = width // n, hidden // n // 2
+    anywhere = pl.BlockSpec(memory_space=pl.ANY)
+    state = pltpu.VMEM((tokens, width), BF16)
+    turned = pltpu.VMEM((width, tokens), BF16)
+    hiddens = pltpu.VMEM((tokens, chunk), BF16)
+    outs = pl.pallas_call(
+        functools.partial(gradients_kernel, n),
+        out_shape=[
+            jax.ShapeDtypeStruct((layers, rows, hidden), BF16),
+            jax.ShapeDtypeStruct((layers, rows, hidden), BF16),
+            jax.ShapeDtypeStruct((layers, 2 * deep, width), BF16),
+            jax.ShapeDtypeStruct((8, 128), F32),
+        ],
+        in_specs=[anywhere] * 5,
+        out_specs=[anywhere] * 3 + [pl.BlockSpec(memory_space=pltpu.VMEM)],
+        scratch_shapes=[
+            state, state, turned, state, turned,
+            pltpu.VMEM((tokens, width), F32),
+            pltpu.VMEM((2, width, chunk), BF16),
+            pltpu.VMEM((2, width, chunk), BF16),
+            pltpu.VMEM((2, chunk, width), BF16),
+            hiddens, hiddens, hiddens,
+            pltpu.VMEM(wg.shape, BF16),
+            pltpu.VMEM(wu.shape, BF16),
+            pltpu.VMEM(wd.shape, BF16),
+            pltpu.VMEM((2, 4, n - 1, rows, wide_cols), BF16),
+            pltpu.VMEM((2, 2, n - 1, deep, width // 2), BF16),
+            pltpu.SemaphoreType.DMA((2, 3)),
+            pltpu.SemaphoreType.DMA((2,)),
+            pltpu.SemaphoreType.DMA((3,)),
+            pltpu.SemaphoreType.DMA((2, 6)),
+            pltpu.SemaphoreType.DMA((2, 6, n - 1)),
+            pltpu.SemaphoreType.REGULAR((2, 6)),
+        ],
+        compiler_params=pltpu.CompilerParams(collective_id=0, has_side_effects=True, vmem_limit_bytes=67_043_328),
+        name="gradients",
+    )(x, dy, *w)
+    return outs[:3], outs[3]
 
 
 def update_kernel(n, layers, count, *refs):
@@ -161,11 +450,7 @@
 
     def device(x, dy, *arrays):
         w, m, v = (arrays[i : i + 3] for i in (0, 3, 6))
-        _, back = jax.vjp(lambda w: stack(w, x[0]), dict(zip(NAMES, w, strict=True)))
-        by_weights = back(dy[0])[0]
-        g = [lax.psum_scatter(by_weights[name], "dp", scatter_dimension=1, tiled=True) for name in NAMES]
-        ssq = sum(jnp.sum(jnp.square(t.astype(F32))) for t in g)
-        ssq = jnp.zeros((8, 128), F32).at[0, 0].set(ssq)
+        g, ssq = gradients(n, x[0], dy[0], w)
         return update(n, ssq, g, w, m, v)
 
     whole, part = P(None, None, None), P(None, "dp", None)

time: 639 us -> 497 us (0.78); the launches traced: 632 us -> 497 us
  Pallas kernels: 190 us -> 468 us
  matrix products: 213 us -> 0 us
  waiting for transfers between devices: 148 us -> 0 us
  other arithmetic: 26.2 us -> 0 us
  between operations: 16.1 us -> 0.68 us
  local copies, waits for them, and re-layouts: 38 us -> 28.4 us
    pallas_call x0 -> x1, Pallas kernels: none -> 283 us  [gradients(): pl.pallas_call(functools.partial(gradients_kernel, n), out_shape=[jax.Sha...]
    dot_general x15 -> x0, matrix products: 213 us -> none  [the longest x5 80.9 us: layer(): gate = jnp.dot(a, w['w_gate'], preferred_element_type=F32)]
    reduce_scatter x3 -> x0, waiting for transfers between devices: 148 us -> none  [device(): lax.psum_scatter(by_weights[name], 'dp', scatter_dimension=1, tiled=True)]
    add_any x4 -> x0, other arithmetic: 19.1 us -> none  [the longest x3 14.1 us: stack(): h = layer(h, {name: w[number] for name, w in weights.items()})]
    unnamed x49 -> x21, local copies, waits for them, and re-layouts: 38 us -> 28.4 us
    reduce_sum x4 -> x0, other arithmetic: 7.09 us -> none  [the longest x3 6.43 us: device(): ssq = sum((jnp.sum(jnp.square(t.astype(F32))) for t in g))]
  transfers between devices with their start and end apart: 3 -> 0, of which waited for: 3 -> 0; matrix products, arithmetic and copies ran while one was open for 12% -> 0% of each run, Pallas kernels for 0% -> 0%
where the time goes in v2:
time: 497 us
  Pallas kernels  468 us (94%)
  local copies, waits for them, and re-layouts  28.4 us (6%)
    pallas_call x1, Pallas kernels, gradients(): pl.pallas_call(functools.partial(gradients_kernel, n), out_shape=[jax.Sha...  283 us
    pallas_call x1, Pallas kernels, update(): pl.pallas_call(functools.partial(update_kernel, n, layers, count), out_sh...  185 us
    unnamed x21, local copies, waits for them, and re-layouts  28.4 us

profile of v2, /device:TPU:22, one launch (start us, length us, event | category | flops | bytes accessed | tf_op | source)
XLA Modules:
  0.0 496.8 jit_solution(9597182030636364098)
XLA Ops:
  0.6 282.5 %gradients.1 = (bf16[2,96,2048]{2,1,0:T(8,128)(2,1)}, bf16[2,96,2048]{2,1,0:T(8,128)(2,1)}, bf16[2,256,768]{2,1,0:T(8,128)(2,1)}, f32[8,128]{1,0:T(8,128)}) custom-call(bf16[2048,768]{1,0:T(8,128)(2,1)} %bitcast.2, bf16[2048,768]{1,0:T(8,128)(2,1)} %bitcast.3, bf16[2,768,2048]{2,1,0:T(8,128)(2,1)} %refs_4_.3, bf16[2,768,2048]{2,1,0:T(8,128)(2,1)} %refs_5_.1, ...), custom_call_target="tpu_custom_call" | custom-call | tf_op jit(solution)/shard_map/gradients/pallas_call | solution.py:292
  283.2 0.0 copy-start
  283.2 1.4 copy-done
  284.6 0.0 copy-start.1
  284.6 1.1 copy-done.1
  285.7 0.0 copy-start.2
  285.7 1.1 copy-done.2
  286.9 0.0 copy-start.3
  286.9 1.1 copy-done.3
  288.0 0.0 copy-start.4
  288.0 0.7 copy-done.4
  288.7 185.2 %update.1 = (bf16[2,768,2048]{2,1,0:T(8,128)(2,1)}, bf16[2,768,2048]{2,1,0:T(8,128)(2,1)}, bf16[2,2048,768]{2,1,0:T(8,128)(2,1)}, f32[2,96,2048]{2,1,0:T(8,128)S...) custom-call(f32[8,128]{1,0:T(8,128)S(1)} %copy-done.4, ...), custom_call_target="tpu_custom_call" | custom-call | tf_op jit(solution)/shard_map/update/pallas_call | solution.py:426
  473.9 6.6 %copy.29 = bf16[2,768,2048]{2,1,0:T(8,128)(2,1)} copy(bf16[2,768,2048]{2,1,0:T(8,128)(2,1)} %get-tuple-element.26) | data formatting | bytes 12582912
  480.5 0.0 copy-start.5
  480.5 6.8 %copy.30 = bf16[2,768,2048]{2,1,0:T(8,128)(2,1)} copy(bf16[2,768,2048]{2,1,0:T(8,128)(2,1)} %get-tuple-element.27) | data formatting | bytes 12582912
  487.2 0.0 copy-done.5
  487.2 2.7 copy.31
  490.0 1.1 copy.32
  491.1 1.1 copy.33
  492.2 1.1 copy.34
  493.4 1.1 copy.35
  494.5 1.1 copy.36
  495.7 1.1 copy.37
Async XLA Ops:
  283.2 1.4 copy-start
  284.6 1.1 copy-start.1
  285.7 1.1 copy-start.2
  286.9 1.1 copy-start.3
  288.0 0.7 copy-start.4
  480.5 6.8 %copy-start.5 = (bf16[2,2048,768]{2,1,0:T(8,128)(2,1)S(1)}, bf16[2,2048,768]{2,1,0:T(8,128)(2,1)}, u32[]{:S(2)}) copy-start(bf16[2,2048,768]{2,1,0:T(8,128)(2,1)} %get-tuple-element.28) | copy-start | bytes 18874372

commit v3 on v2

--- a/solution.py
+++ b/solution.py
@@ -8,7 +8,7 @@
 from jax.sharding import PartitionSpec as P
 
 MESH = pl.DeviceIdType.MESH
-STARTS = (4, 8, 12, 16, 16, 16, 20, 22, 24, 26, 26, 26)
+STARTS = (3, 6, 9, 12, 12, 12, 17, 18, 20, 22, 22, 22)
 F32, BF16 = jnp.float32, jnp.bfloat16
 
 
@@ -175,11 +175,12 @@
                     for way in range(2):
                         pl.semaphore_signal(credit.at[way, lane], inc=1, device_id={"dp": (left, right)[way]}, device_id_type=MESH)
 
-    def lane(which, step):
+    def lane(which, step, now=True):
         first, second = STARTS[which], STARTS[which + 6]
         later = step >= second
         s = step - jnp.where(later, second, first)
-        serve(0 if which < 4 else 1, which, jnp.where(later, which + 6, which), s, jnp.logical_and(s >= 0, s <= n - 1))
+        due = jnp.logical_and(jnp.logical_and(s >= 0, s <= n - 1), now)
+        serve(0 if which < 4 else 1, which, jnp.where(later, which + 6, which), s, due)
 
     def backward(number, count, rounds):
         t = chunks + count
@@ -209,19 +210,22 @@
         rounds(6)
 
     def last_layer(count, _):
+        pair, odd = lax.div(count, 2), lax.rem(count, 2)
+
         def rounds(place):
-            if place not in (0, 4):
-                which = {1: 0, 2: 1, 3: 2, 5: 0, 6: 1}[place]
-                lane(which, 2 * count + (place > 3))
-            if place == 6:
-                lane(2, 2 * count + 1)
+            for which in (0, 1, 2):
+                if place == 3:
+                    lane(which, 3 * pair + 2 * odd)
+                if place == 6:
+                    lane(which, 3 * pair + 1, odd == 0)
 
         backward(1, count, rounds)
         return 0
 
     lax.fori_loop(0, chunks, last_layer, 0)
-    for which in (2, 3, 4, 5):
-        lane(which, 2 * chunks)
+    middle = 3 * chunks // 2
+    for which in (1, 2, 3, 4, 5):
+        lane(which, middle)
 
     def through_norm(i, _):
         part = tokens_at(i)
@@ -236,8 +240,8 @@
     lax.fori_loop(0, 4, through_norm, 0)
     load_x = pltpu.make_async_copy(x, h, xsem.at[0])
     load_x.start()
-    for which in (2, 3, 4, 5):
-        lane(which, 2 * chunks + 1)
+    for which in (1, 2, 3, 4, 5):
+        lane(which, middle + 1)
     load_x.wait()
     norm_all()
 
@@ -250,9 +254,8 @@
 
     def first_layer(count, _):
         def rounds(place):
-            which = {0: 2, 1: 3, 2: 4, 3: 5, 5: 0, 6: 1}.get(place)
-            if which is not None:
-                lane(which, chunks + 2 + count)
+            for which in {3: (2, 3, 4), 6: (5, 0, 1)}.get(place, ()):
+                lane(which, middle + 2 + count - chunks)
 
         backward(0, count, rounds)
         return 0
@@ -264,7 +267,7 @@
             lane(which, step)
         return 0
 
-    lax.fori_loop(3 * chunks + 2, 3 * chunks + 10, rest, 0)
+    lax.fori_loop(middle + 2 + chunks, middle + 2 + chunks + n, rest, 0)
 
     own = pl.ds(pl.multiple_of(me * rows, rows), rows)
     own_deep = pl.ds(pl.multiple_of(me * 2 * deep, 2 * deep), 2 * deep)
@@ -423,10 +426,11 @@
     count = float(sum(t.size for t in w))
     blocks = 3 * layers
     anywhere = pl.BlockSpec(memory_space=pl.ANY)
+    g, w, m, v = ([pltpu.with_memory_space_constraint(t, pltpu.HBM) for t in ts] for ts in (g, w, m, v))
     outs = pl.pallas_call(
         functools.partial(update_kernel, n, layers, count),
         out_shape=[jax.ShapeDtypeStruct(t.shape, t.dtype) for t in (*w, *m, *v)],
-        in_specs=[pl.BlockSpec(memory_space=pltpu.VMEM)] + [anywhere] * 12,
+        in_specs=[pl.BlockSpec(memory_space=pltpu.VMEM)] + [pl.BlockSpec(memory_space=pltpu.HBM)] * 12,
         out_specs=[anywhere] * 9,
         scratch_shapes=[pltpu.VMEM(t.shape, t.dtype) for t in (*g, *g, *m, *v)]
         + [
@@ -439,19 +443,42 @@
             pltpu.SemaphoreType.DMA((2, blocks, n - 1)),
             pltpu.SemaphoreType.DMA((2, blocks, n - 1)),
         ],
-        compiler_params=pltpu.CompilerParams(collective_id=1, has_side_effects=True, vmem_limit_bytes=40 * 2**20),
+        compiler_params=pltpu.CompilerParams(collective_id=1, has_side_effects=True, vmem_limit_bytes=16 * 2**20),
         name="update",
     )(ssq, *g, *w, *m, *v)
     return tuple(outs)
 
 
+def settle_kernel(*refs):
+    *arrays, sems = refs
+    half = len(arrays) // 2
+    copies = [pltpu.make_async_copy(arrays[k], arrays[half + k], sems.at[k]) for k in range(half)]
+    for copy in copies:
+        copy.start()
+    for copy in copies:
+        copy.wait()
+
+
+def settle(results):
+    anywhere = pl.BlockSpec(memory_space=pl.ANY)
+    return pl.pallas_call(
+        settle_kernel,
+        out_shape=[jax.ShapeDtypeStruct(t.shape, t.dtype) for t in results],
+        in_specs=[anywhere] * len(results),
+        out_specs=[anywhere] * len(results),
+        scratch_shapes=[pltpu.SemaphoreType.DMA((len(results),))],
+        compiler_params=pltpu.CompilerParams(vmem_limit_bytes=2**20),
+        name="settle",
+    )(*results)
+
+
 def solution(mesh):
     n = mesh.shape["dp"]
 
     def device(x, dy, *arrays):
         w, m, v = (arrays[i : i + 3] for i in (0, 3, 6))
         g, ssq = gradients(n, x[0], dy[0], w)
-        return update(n, ssq, g, w, m, v)
+        return tuple(settle(update(n, ssq, g, w, m, v)))
 
     whole, part = P(None, None, None), P(None, "dp", None)
     return jax.shard_map(

time: 497 us -> 459 us (0.924)
  local copies, waits for them, and re-layouts: 28.4 us -> 0.65 us
  Pallas kernels: 468 us -> 457 us
    unnamed x21 -> x2, local copies, waits for them, and re-layouts: 28.4 us -> 0.65 us
    pallas_call x1, Pallas kernels: 283 us -> 265 us  [gradients(): pl.pallas_call(functools.partial(gradients_kernel, n), out_shape=[jax.Sha...]
    pallas_call x0 -> x1, Pallas kernels: none -> 9.45 us  [settle(): pl.pallas_call(settle_kernel, out_shape=[jax.ShapeDtypeStruct(t.shape, t....]
where the time goes in v3:
time: 459 us
  Pallas kernels  457 us (100%)
    pallas_call x1, Pallas kernels, gradients(): pl.pallas_call(functools.partial(gradients_kernel, n), out_shape=[jax.Sha...  265 us
    pallas_call x1, Pallas kernels, update(): pl.pallas_call(functools.partial(update_kernel, n, layers, count), out_sh...  182 us
    pallas_call x1, Pallas kernels, settle(): pl.pallas_call(settle_kernel, out_shape=[jax.ShapeDtypeStruct(t.shape, t....  9.45 us

profile of v3, /device:TPU:22, one launch (start us, length us, event | category | flops | bytes accessed | tf_op | source)
XLA Modules:
  0.0 458.8 jit_solution(11584233435326334407)
XLA Ops:
  0.6 265.4 %gradients.1 = (bf16[2,96,2048]{2,1,0:T(8,128)(2,1)}, bf16[2,96,2048]{2,1,0:T(8,128)(2,1)}, bf16[2,256,768]{2,1,0:T(8,128)(2,1)}, f32[8,128]{1,0:T(8,128)}) custom-call(bf16[2048,768]{1,0:T(8,128)(2,1)} %bitcast.2, bf16[2048,768]{1,0:T(8,128)(2,1)} %bitcast.3, bf16[2,768,2048]{2,1,0:T(8,128)(2,1)} %refs_4_.3, bf16[2,768,2048]{2,1,0:T(8,128)(2,1)} %refs_5_.1, ...), custom_call_target="tpu_custom_call" | custom-call | tf_op jit(solution)/shard_map/gradients/pallas_call | solution.py:295
  266.1 0.0 copy-start
  266.1 0.7 copy-done
  266.7 182.5 %update.1 = (bf16[2,768,2048]{2,1,0:T(8,128)(2,1)S(1)}, bf16[2,768,2048]{2,1,0:T(8,128)(2,1)S(1)}, bf16[2,2048,768]{2,1,0:T(8,128)(2,1)S(1)}, f32[2,96,2048]{2,1...) custom-call(f32[8,128]{1,0:T(8,128)S(1)} %copy-done, ...), custom_call_target="tpu_custom_call" | custom-call | tf_op jit(solution)/shard_map/update/pallas_call | solution.py:430
  449.2 9.4 %settle.1 = (bf16[2,768,2048]{2,1,0:T(8,128)(2,1)}, bf16[2,768,2048]{2,1,0:T(8,128)(2,1)}, bf16[2,2048,768]{2,1,0:T(8,128)(2,1)}, f32[2,96,2048]{2,1,0:T(8,128)}...) custom-call(bf16[2,768,2048]{2,1,0:T(8,128)(2,1)S(1)} %get-tuple-ele, ...), custom_call_target="tpu_custom_call" | custom-call | tf_op jit(solution)/shard_map/settle/pallas_call | solution.py:464
Async XLA Ops:
  266.1 0.7 copy-start

commit v4 on v3

--- a/solution.py
+++ b/solution.py
@@ -8,7 +8,7 @@
 from jax.sharding import PartitionSpec as P
 
 MESH = pl.DeviceIdType.MESH
-STARTS = (3, 6, 9, 12, 12, 12, 17, 18, 20, 22, 22, 22)
+STARTS = (1, 3, 5, 7, 7, 7, 12, 14, 16, 19, 19, 19)
 F32, BF16 = jnp.float32, jnp.bfloat16
 
 
@@ -25,9 +25,9 @@
 
 
 def gradients_kernel(n, *refs):
-    x, dy, wg, wu, wd, og, ou, od, ossq = refs[:9]
-    h, a, at, d, dt, acc, wgb, wub, wdb, act, dg, du, gg, gu, gd, rgu, rd = refs[9:26]
-    wsem, xsem, osem, send_sem, recv_sem, credit = refs[26:]
+    x, dy, wg, wu, wd, og, ou, od, ossq, spill = refs[:10]
+    h, a, at, d, dt, acc, wgb, wub, wdb, act, dg, du, gg, gu, gd, rgu, rd = refs[10:27]
+    wsem, xsem, osem, send_sem, recv_sem, credit, spill_sem = refs[27:]
     me = lax.axis_index("dp")
     right, left = lax.rem(me + 1, n), lax.rem(me + n - 1, n)
     tokens, width = h.shape
@@ -42,7 +42,7 @@
         return pl.ds(pl.multiple_of(i * tile, tile), tile)
 
     def chunk_of(t):
-        number = jnp.where(lax.div(t, chunks) == 1, 1, 0)
+        number = jnp.where(jnp.logical_or(lax.div(t, chunks) == 1, lax.div(t, chunks) == 2), 1, 0)
         cols = pl.ds(pl.multiple_of(lax.rem(t, chunks) * chunk, chunk), chunk)
         slot = lax.rem(t, 2)
         return [
@@ -88,7 +88,7 @@
     load_dy.wait()
 
     def forward(t, _):
-        next_chunk(t, 3 * chunks - 1)
+        next_chunk(t, 4 * chunks - 1)
         slot = lax.rem(t, 2)
         turn(d, dt, t, tokens // chunks)
         for i in range(4):
@@ -182,11 +182,26 @@
         due = jnp.logical_and(jnp.logical_and(s >= 0, s <= n - 1), now)
         serve(0 if which < 4 else 1, which, jnp.where(later, which + 6, which), s, due)
 
+    def kept(count):
+        slot = lax.rem(count, 2)
+        return [pltpu.make_async_copy(ref.at[slot], spill.at[k, count], spill_sem.at[k, slot]) for k, ref in enumerate((dg, du))]
+
+    def again(count):
+        slot = lax.rem(count, 2)
+        return [pltpu.make_async_copy(spill.at[k, count], ref.at[slot], spill_sem.at[k, slot]) for k, ref in enumerate((dg, du))]
+
     def backward(number, count, rounds):
-        t = chunks + count
-        next_chunk(t, 3 * chunks - 1)
+        t = jnp.where(count < chunks, chunks, 2 * chunks) + count
+        next_chunk(t, 4 * chunks - 1)
         slot = lax.rem(t, 2)
         cols = pl.ds(pl.multiple_of(lax.rem(count, chunks) * chunk, chunk), chunk)
+        if number == 1:
+
+            @pl.when(count >= 2)
+            def _():
+                for copy in kept(count - 2):
+                    copy.wait()
+
         for i in range(4):
             part = pl.ds(i * tile, tile)
             gate = nn(a[part, :], wgb[slot])
@@ -197,35 +212,61 @@
             act[part, :] = (silu * up).astype(BF16)
             by_up = (back * silu).astype(BF16)
             by_gate = (back * up * (sig + silu * (1.0 - sig))).astype(BF16)
-            du[part, :] = by_up
-            dg[part, :] = by_gate
-            if number == 1:
-                acc[part, :] += nt(by_gate, wgb[slot]) + nt(by_up, wub[slot])
+            du[slot, part, :] = by_up
+            dg[slot, part, :] = by_gate
             rounds(i)
-        gg[number, :, cols] = nn(at[...], dg[...]).astype(BF16)
+        gg[number, :, cols] = nn(at[...], dg[slot]).astype(BF16)
         rounds(4)
-        gu[number, :, cols] = nn(at[...], du[...]).astype(BF16)
+        gu[number, :, cols] = nn(at[...], du[slot]).astype(BF16)
         rounds(5)
         gd[number, cols, :] = nn(dt[...], act[...]).T.astype(BF16)
+        if number == 1:
+            for copy in kept(count):
+                copy.start()
         rounds(6)
 
     def last_layer(count, _):
-        pair, odd = lax.div(count, 2), lax.rem(count, 2)
-
         def rounds(place):
-            for which in (0, 1, 2):
-                if place == 3:
-                    lane(which, 3 * pair + 2 * odd)
-                if place == 6:
-                    lane(which, 3 * pair + 1, odd == 0)
+            if place == 6:
+                for which in (0, 1, 2):
+                    lane(which, count)
 
         backward(1, count, rounds)
         return 0
 
     lax.fori_loop(0, chunks, last_layer, 0)
-    middle = 3 * chunks // 2
-    for which in (1, 2, 3, 4, 5):
-        lane(which, middle)
+    for which in (3, 4, 5):
+        lane(which, chunks - 1)
+
+    for count in (chunks - 2, chunks - 1):
+        for copy in kept(count):
+            copy.wait()
+    for copy in again(0):
+        copy.start()
+
+    def state_half(half, _):
+        def state(count, _):
+            next_chunk(2 * chunks + count, 4 * chunks - 1)
+            slot = lax.rem(count, 2)
+            for copy in again(count):
+                copy.wait()
+
+            @pl.when(count < chunks - 1)
+            def _():
+                for copy in again(count + 1):
+                    copy.start()
+
+            for i in range(4):
+                part = pl.ds(i * tile, tile)
+                acc[part, :] += nt(dg[slot, part, :], wgb[slot]) + nt(du[slot, part, :], wub[slot])
+            return 0
+
+        lax.fori_loop(half * (chunks // 2), (half + 1) * (chunks // 2), state, 0)
+        for which in (0, 1, 2, 3, 4, 5):
+            lane(which, chunks + half)
+        return 0
+
+    lax.fori_loop(0, 2, state_half, 0)
 
     def through_norm(i, _):
         part = tokens_at(i)
@@ -241,7 +282,7 @@
     load_x = pltpu.make_async_copy(x, h, xsem.at[0])
     load_x.start()
     for which in (1, 2, 3, 4, 5):
-        lane(which, middle + 1)
+        lane(which, chunks + 2)
     load_x.wait()
     norm_all()
 
@@ -254,8 +295,8 @@
 
     def first_layer(count, _):
         def rounds(place):
-            for which in {3: (2, 3, 4), 6: (5, 0, 1)}.get(place, ()):
-                lane(which, middle + 2 + count - chunks)
+            for which in {3: (3, 4, 5), 6: (0, 1, 2)}.get(place, ()):
+                lane(which, 3 + count)
 
         backward(0, count, rounds)
         return 0
@@ -267,7 +308,7 @@
             lane(which, step)
         return 0
 
-    lax.fori_loop(middle + 2 + chunks, middle + 2 + chunks + n, rest, 0)
+    lax.fori_loop(3 + 2 * chunks, 3 + 2 * chunks + n, rest, 0)
 
     own = pl.ds(pl.multiple_of(me * rows, rows), rows)
     own_deep = pl.ds(pl.multiple_of(me * 2 * deep, 2 * deep), 2 * deep)
@@ -299,16 +340,17 @@
             jax.ShapeDtypeStruct((layers, rows, hidden), BF16),
             jax.ShapeDtypeStruct((layers, 2 * deep, width), BF16),
             jax.ShapeDtypeStruct((8, 128), F32),
+            jax.ShapeDtypeStruct((2, hidden // chunk, tokens, chunk), BF16),
         ],
         in_specs=[anywhere] * 5,
-        out_specs=[anywhere] * 3 + [pl.BlockSpec(memory_space=pltpu.VMEM)],
+        out_specs=[anywhere] * 3 + [pl.BlockSpec(memory_space=pltpu.VMEM), anywhere],
         scratch_shapes=[
             state, state, turned, state, turned,
             pltpu.VMEM((tokens, width), F32),
             pltpu.VMEM((2, width, chunk), BF16),
             pltpu.VMEM((2, width, chunk), BF16),
             pltpu.VMEM((2, chunk, width), BF16),
-            hiddens, hiddens, hiddens,
+            hiddens, pltpu.VMEM((2, tokens, chunk), BF16), pltpu.VMEM((2, tokens, chunk), BF16),
             pltpu.VMEM(wg.shape, BF16),
             pltpu.VMEM(wu.shape, BF16),
             pltpu.VMEM(wd.shape, BF16),
@@ -320,6 +362,7 @@
             pltpu.SemaphoreType.DMA((2, 6)),
             pltpu.SemaphoreType.DMA((2, 6, n - 1)),
             pltpu.SemaphoreType.REGULAR((2, 6)),
+            pltpu.SemaphoreType.DMA((2, 2)),
         ],
         compiler_params=pltpu.CompilerParams(collective_id=0, has_side_effects=True, vmem_limit_bytes=67_043_328),
         name="gradients",

time: 459 us -> 441 us (0.961)
  Pallas kernels: 457 us -> 439 us
    pallas_call x1, Pallas kernels: 265 us -> 246 us  [gradients(): pl.pallas_call(functools.partial(gradients_kernel, n), out_shape=[jax.Sha...]
where the time goes in v4:
time: 441 us
  Pallas kernels  439 us (100%)
    pallas_call x1, Pallas kernels, gradients(): pl.pallas_call(functools.partial(gradients_kernel, n), out_shape=[jax.Sha...  246 us
    pallas_call x1, Pallas kernels, update(): pl.pallas_call(functools.partial(update_kernel, n, layers, count), out_sh...  184 us
    pallas_call x1, Pallas kernels, settle(): pl.pallas_call(settle_kernel, out_shape=[jax.ShapeDtypeStruct(t.shape, t....  9.45 us

profile of v4, /device:TPU:22, one launch (start us, length us, event | category | flops | bytes accessed | tf_op | source)
XLA Modules:
  0.0 440.5 jit_solution(8829680723551666181)
XLA Ops:
  0.6 245.7 %gradients.1 = (bf16[2,96,2048]{2,1,0:T(8,128)(2,1)}, bf16[2,96,2048]{2,1,0:T(8,128)(2,1)}, bf16[2,256,768]{2,1,0:T(8,128)(2,1)}, f32[8,128]{1,0:T(8,128)}, bf16[2,8,2048,256]{3,2,1,0:T(8,128)(2,1)}) custom-call(bf16[2048,768]{1,0:T(8,128)(2,1)} %bitcast.2, bf16[2048,768]{1,0:T(8,128)(2,1)} %bitcast.3, bf16[2,768,2048]{2,1,0:T(8,128)(2,1)} %refs_4_.3, ...), custom_call_target="tpu_custom_call" | custom-call | tf_op jit(solution)/shard_map/gradients/pallas_call | solution.py:336
  246.4 0.0 copy-start
  246.4 0.7 copy-done
  247.1 183.9 %update.1 = (bf16[2,768,2048]{2,1,0:T(8,128)(2,1)S(1)}, bf16[2,768,2048]{2,1,0:T(8,128)(2,1)S(1)}, bf16[2,2048,768]{2,1,0:T(8,128)(2,1)S(1)}, f32[2,96,2048]{2,1...) custom-call(f32[8,128]{1,0:T(8,128)S(1)} %copy-done, ...), custom_call_target="tpu_custom_call" | custom-call | tf_op jit(solution)/shard_map/update/pallas_call | solution.py:473
  430.9 9.4 %settle.1 = (bf16[2,768,2048]{2,1,0:T(8,128)(2,1)}, bf16[2,768,2048]{2,1,0:T(8,128)(2,1)}, bf16[2,2048,768]{2,1,0:T(8,128)(2,1)}, f32[2,96,2048]{2,1,0:T(8,128)}...) custom-call(bf16[2,768,2048]{2,1,0:T(8,128)(2,1)S(1)} %get-tuple-ele, ...), custom_call_target="tpu_custom_call" | custom-call | tf_op jit(solution)/shard_map/settle/pallas_call | solution.py:507
Async XLA Ops:
  246.4 0.7 copy-start
